TPU v7x, 256 devices: a whole 4x4x8 slice. The times are simulated.
256 devices in a mesh: dp: 64 (over z_lo, x, y), tensor: 4 (over z_hi, core).
Axes of the slice: x: 4, y: 4, z: 8 (z_hi: 2, z_lo: 4; z = z_hi * 4 + z_lo), core: 2. Of those that a mesh axis runs over, the one named last changes fastest.
Arguments:
- hidden_states: float32 [32768, 2048], P(('dp', 'tensor')), may hold values from -40 to 40
- lengths: int32 [64], P('dp'), may hold values from 128 to 512
- shard_order: int32 [64], replicated, may hold values from 0 to 63, each once
- gain_attn: float32 [2048], replicated, may hold values from 0.25 to 1.75
- w_query: bfloat16 [2048, 2048], P('dp', 'tensor'), may hold values from -0.015625 to 0.015625
- w_key: bfloat16 [2048, 2048], P('dp', 'tensor'), may hold values from -0.125 to 0.125
- w_value: bfloat16 [2048, 2048], P('dp', 'tensor'), may hold values from -0.125 to 0.125
- w_out: bfloat16 [2048, 2048], P('tensor', 'dp'), may hold values from -1 to 1
- rel_bias: float32 [32, 32], P(None, 'tensor'), may hold values from -6 to 300
- gain_ff: float32 [2048], replicated, may hold values from 0.25 to 1.75
- w_gate: bfloat16 [2048, 5120], P('dp', 'tensor'), may hold values from -0.125 to 0.125
- w_up: bfloat16 [2048, 5120], P('dp', 'tensor'), may hold values from -0.125 to 0.125
- w_down: bfloat16 [5120, 2048], P('tensor', 'dp'), may hold values from -0.078125 to 0.078125
- gain_final: float32 [2048], replicated, may hold values from 0.25 to 1.75
- w_reward: float32 [2048], replicated, may hold values from -0.125 to 0.125
Outputs:
- layer_output: float32 [32768, 2048], P(('dp', 'tensor'))
- normalized_rewards: float32 [64], P('dp')
Inputs may be any that keep to these rules, and one draw needn't show every extreme that they name: `shard_order`: each of 0 to 64 - 1 appears once. `lengths`: positions at or beyond a rollout's length are padding.
All inputs are finite; a program needn't handle non-finite values.
Results may differ from a plain program's by a relative error of at most 0.02.
Values may be sent and summed in bfloat16 or wider, within the bound.
A program may use at most 128 MiB of HBM per device.

v0:
```python
import jax
import jax.numpy as jnp
from jax import lax
from jax.sharding import PartitionSpec as P

DK = 64
LEN = 512
bucket_edges = (12, 16, 23, 32, 46, 64, 91)


def in_order(parts, dim):
    parts = jnp.moveaxis(parts, 0, dim)
    shape = parts.shape
    return parts.reshape(*shape[:dim], shape[dim] * shape[dim + 1], *shape[dim + 2 :])


def from_everyone(array, axis):
    peers = lax.axis_size(axis)
    return lax.all_to_all(
        jnp.broadcast_to(array[None], (peers, *array.shape)), axis, 0, 0, tiled=True
    )


def gather_directly(array, axis, dim):
    return in_order(from_everyone(array, axis), dim)


def in_one_piece(arrays, axis, dim, along):
    ends, at = ([], 0)
    for a in arrays[:-1]:
        at += a.shape[along]
        ends.append(at)
    both = jnp.concatenate(arrays, axis=along)
    return tuple(jnp.split(lax.all_gather(both, axis, axis=dim, tiled=True), ends, axis=along))


def cut_along(array, dim, peers):
    shape = array.shape
    parts = array.reshape(*shape[:dim], peers, shape[dim] // peers, *shape[dim + 1 :])
    return jnp.moveaxis(parts, dim, 0)


def sent_and_summed(array, axis, dim):
    peers = lax.axis_size(axis)
    parts = lax.all_to_all(cut_along(array, dim, peers), axis, 0, 0, tiled=True)
    return jnp.sum(parts.astype(jnp.float32), axis=0)


def of_everyone(array, axis):
    return from_everyone(array, axis).sum(axis=0)


def packed_total(arrays, axis):
    line, at, gathered = (jnp.concatenate([a.reshape(-1) for a in arrays]), 0, [])
    running = of_everyone(line, axis)
    for a in arrays:
        gathered.append(running[at : at + a.size].reshape(a.shape))
        at += a.size
    return tuple(gathered)


def bucket_index(relative):
    distance = jnp.abs(relative)
    bucket_low = jnp.minimum(distance, 8)
    for threshold in bucket_edges:
        bucket_low = bucket_low + (distance >= threshold).astype(jnp.int32)
    return jnp.where(relative > 0, 16, 0) + bucket_low


def rms_norm(values_in, weight_gain):
    return (
        values_in
        * lax.rsqrt(jnp.mean(values_in * values_in, axis=-1, keepdims=True) + 1e-06)
        * weight_gain
    )


def reorder_blocks(values_in, ordering):
    full_shape = values_in.shape
    blocks = values_in.reshape(
        full_shape[:-1] + (ordering.shape[0], full_shape[-1] // ordering.shape[0])
    )
    return jnp.take(blocks, ordering, axis=-2).reshape(full_shape)


def local(
    hidden_states,
    lengths,
    shard_order,
    gain_attn,
    w_query,
    w_key,
    w_value,
    w_out,
    rel_bias,
    gain_ff,
    w_gate,
    w_up,
    w_down,
    gain_final,
    w_reward,
):
    groups = shard_order.shape[0]
    block_ids = jnp.arange(groups, dtype=jnp.int32)
    inverse = jnp.sum(
        block_ids[:, None] * (shard_order[:, None] == block_ids[None, :]).astype(jnp.int32), axis=0
    )
    own_rows = reorder_blocks(hidden_states, shard_order)
    attn_gain = reorder_blocks(gain_attn, shard_order)
    feed_gain = reorder_blocks(gain_ff, shard_order)
    final_gain = reorder_blocks(gain_final, shard_order)
    reward_head = reorder_blocks(w_reward, shard_order)
    row_count = own_rows.shape[0]
    row_start = lax.axis_index("tensor") * row_count
    normed = gather_directly(rms_norm(own_rows, attn_gain).astype(jnp.bfloat16), "tensor", 0)

    def contract_with(source):

        def contract(running, portion, offset):
            return jnp.dot(source, portion, preferred_element_type=jnp.float32)

        return contract

    inner_width = w_query.shape[1]
    zero_block = jnp.zeros((LEN, inner_width), jnp.float32)
    attn_contract = contract_with(normed)
    running = (zero_block, zero_block, zero_block)
    portion = in_one_piece((w_query, w_key, w_value), "dp", 0, 1)
    offset = jnp.int32(0)
    queries = attn_contract(running[0], portion[0], offset)
    key_states = attn_contract(running[1], portion[1], offset)
    value_states = attn_contract(running[2], portion[2], offset)
    head_count = inner_width // DK
    query_heads = queries.astype(jnp.bfloat16).reshape(LEN, head_count, DK).transpose(1, 0, 2)
    key_heads = key_states.astype(jnp.bfloat16).reshape(LEN, head_count, DK).transpose(1, 0, 2)
    value_heads = value_states.astype(jnp.bfloat16).reshape(LEN, head_count, DK).transpose(1, 0, 2)
    span = 2 * LEN - 1
    offsets = jnp.arange(span, dtype=jnp.int32)
    relative = jnp.where(offsets < LEN, offsets, offsets - span)
    bucket_ids = bucket_index(relative)
    onehot = (
        bucket_ids[:, None] == jnp.arange(rel_bias.shape[0], dtype=jnp.int32)[None, :]
    ).astype(jnp.float32)
    offset_bias = jnp.dot(onehot, rel_bias, precision=lax.Precision.HIGHEST).T
    length = lengths[0]
    in_range = jnp.arange(LEN, dtype=jnp.int32) < length

    def head_step(operands):
        head_query, head_key, head_value, head_offsets = operands
        repeated = jnp.tile(head_offsets, LEN)[: LEN * (span - 1)].reshape(LEN, span - 1)[:, :LEN]
        scores = jnp.dot(head_query, head_key.T, preferred_element_type=jnp.float32) + repeated
        scores = jnp.where(in_range[None, :], scores, -1e30)
        row_max = jnp.max(scores, axis=-1, keepdims=True)
        exp_scores = jnp.exp(scores - row_max)
        soft_weights = (exp_scores / jnp.sum(exp_scores, axis=-1, keepdims=True)).astype(
            jnp.bfloat16
        )
        return jnp.dot(soft_weights, head_value, preferred_element_type=jnp.float32).astype(
            jnp.bfloat16
        )

    context = lax.map(head_step, (query_heads, key_heads, value_heads, offset_bias))
    context = context.transpose(1, 0, 2).reshape(LEN, inner_width)
    attn_partial = jnp.dot(
        context, lax.all_gather(w_out, "dp", axis=1, tiled=True), preferred_element_type=jnp.float32
    ).astype(jnp.bfloat16)
    mid_own = own_rows + sent_and_summed(attn_partial, "tensor", 0)
    mid_normed = gather_directly(rms_norm(mid_own, feed_gain).astype(jnp.bfloat16), "tensor", 0)
    hidden_width = w_gate.shape[1]
    zero_hidden = jnp.zeros((LEN, hidden_width), jnp.float32)
    feed_contract = contract_with(mid_normed)
    running = (zero_hidden, zero_hidden)
    portion = in_one_piece((w_gate, w_up), "dp", 0, 1)
    offset = jnp.int32(0)
    gate_proj = feed_contract(running[0], portion[0], offset)
    up_proj = feed_contract(running[1], portion[1], offset)
    activated = (jax.nn.gelu(gate_proj, approximate=True) * up_proj).astype(jnp.bfloat16)
    feed_partial = jnp.dot(
        activated,
        lax.all_gather(w_down, "dp", axis=1, tiled=True),
        preferred_element_type=jnp.float32,
    ).astype(jnp.bfloat16)
    output_rows = mid_own + lax.psum_scatter(
        feed_partial, "tensor", scatter_dimension=0, tiled=True
    ).astype(jnp.float32)
    final_normed = rms_norm(output_rows, final_gain)
    token_score = jnp.dot(final_normed, reward_head, precision=lax.Precision.HIGHEST)
    positions = row_start + jnp.arange(row_count, dtype=jnp.int32)
    local_pool = jnp.sum(jnp.where(positions < length, token_score, 0.0))
    pooled_sum = of_everyone(local_pool, "tensor")
    reward = jnp.reshape(pooled_sum / length.astype(jnp.float32), (1,))
    rollouts = lax.axis_size("dp") * lengths.shape[0]
    first_moment, second_moment = packed_total((jnp.sum(reward), jnp.sum(reward * reward)), "dp")
    reward_mean = first_moment / rollouts
    reward_var = second_moment / rollouts - reward_mean * reward_mean
    normalized = (reward - reward_mean) / jnp.sqrt(reward_var + 1e-06)
    return (reorder_blocks(output_rows, inverse), normalized)


def solution(mesh):
    placed = (
        P(("dp", "tensor"), None),
        P("dp"),
        P(),
        P(),
        P("dp", "tensor"),
        P("dp", "tensor"),
        P("dp", "tensor"),
        P("tensor", "dp"),
        P(None, "tensor"),
        P(),
        P("dp", "tensor"),
        P("dp", "tensor"),
        P("tensor", "dp"),
        P(),
        P(),
    )
    return jax.shard_map(
        local,
        mesh=mesh,
        in_specs=placed,
        out_specs=(P(("dp", "tensor"), None), P("dp")),
        check_vma=False,
    )
```

profile of v0, /device:TPU:1, one launch (start us, length us, event | category | flops | bytes accessed | tf_op | source)
XLA Modules:
  0.0 1597.9 jit_solution(13214527331848942773)
XLA Ops:
  21.1 9.9 all-to-all-start
  32.1 48.3 %all-to-all-done = bf16[4,128,2048]{2,1,0:T(8,128)(2,1)S(1)} async-done(((bf16[4,128,2048]{2,1,0:T(8,128)(2,1)}), bf16[4,128,2048]{2,1,0:T(8,128)(2,1)S(1)}, u32[]{:S(2)}, u32[]{:S(2)}) %all-to-all-start) | async-done | bytes 2097184 | tf_op jit(solution)/shard_map/all_to_all | solution.py:19
  80.5 256.9 %all-gather.5.cloned.1.call-done = bf16[2048,1536]{1,0:T(8,128)(2,1)} async-done(((bf16[32,1536]{1,0:T(8,128)(2,1)}), bf16[2048,1536]{1,0:T(8,128)(2,1)}) %all-gather.5.cloned.1.call-update) | async-done | bytes 6291472 | tf_op jit(solution)/shard_map/all_gather | solution.py:34
  337.3 3.7 fusion.39
  341.0 2.4 copy.43
  343.4 3.7 fusion.42
  347.1 2.4 copy.44
  349.5 3.7 fusion.45
  353.2 2.4 copy.45
  355.7 103.8 %while.11 = (s32[]{:T(128)}, bf16[8,512,64]{1,2,0:T(8,128)(2,1)}, bf16[8,512,64]{2,1,0:T(8,128)(2,1)}, bf16[8,512,64]{2,1,0:T(8,128)(2,1)}, f32[8,1023]{1,0:T(8,...) while((s32[]{:T(128)}, bf16[8,512,64]{1,2,0:T(8,128)(2,1)}, ...), condition=%wide.region_4.7_spmd.clone, body=%wide.region_1.6_spmd.clone.sunk | while | flops 69238272 | bytes 26672264 | solution.py:162
  355.9 2.7 tile.17
  360.2 2.9 reshape.327
  366.8 1.9 fusion.90
  368.9 2.7 tile.17
  373.2 2.9 reshape.327
  379.8 1.8 fusion.90
  381.9 2.7 tile.17
  386.2 2.9 reshape.327
  392.8 1.8 fusion.90
  394.9 2.7 tile.17
  399.1 2.9 reshape.327
  407.8 2.7 tile.17
  412.1 2.9 reshape.327
  418.7 1.8 fusion.90
  420.8 2.7 tile.17
  425.1 2.9 reshape.327
  431.7 1.8 fusion.90
  433.8 2.7 tile.17
  438.1 2.9 reshape.327
  444.7 1.8 fusion.90
  446.8 2.7 tile.17
  451.0 2.9 reshape.327
  457.6 1.8 fusion.90
  459.5 227.3 %all-gather.7.cloned.1.call-done = bf16[512,2048]{0,1:T(8,128)(2,1)} async-done(((bf16[512,32]{0,1:T(8,128)(2,1)}), bf16[512,2048]{0,1:T(8,128)(2,1)}) %all-gather.7.cloned.1.call-update) | async-done | bytes 2097168 | tf_op jit(solution)/shard_map/all_gather | solution.py:165
  686.8 4.4 convolution_convert_fusion.2
  691.2 86.6 %all-to-all-start.1 = ((bf16[4,128,2048]{2,1,0:T(8,128)(2,1)}), bf16[4,128,2048]{2,1,0:T(8,128)(2,1)}, u32[]{:S(2)}, u32[]{:S(2)}) async-start(bf16[4,128,2048]{2,1,0:T(8,128)(2,1)} %bitcast.15), calls=%async_computation.1 | async-start | bytes 4194304 | tf_op jit(solution)/shard_map/all_to_all | solution.py:45
  779.3 36.6 %all-to-all-done.1 = bf16[4,128,2048]{2,1,0:T(8,128)(2,1)} async-done(((bf16[4,128,2048]{2,1,0:T(8,128)(2,1)}), bf16[4,128,2048]{2,1,0:T(8,128)(2,1)}, u32[]{:S(2)}, u32[]{:S(2)}) %all-to-all-start.1) | async-done | bytes 2097184 | tf_op jit(solution)/shard_map/all_to_all | solution.py:45
  815.9 2.1 convert_reduce_fusion
  820.1 44.2 %all_to_all.27 = bf16[4,128,2048]{2,1,0:T(8,128)(2,1)} all-to-all(bf16[4,128,2048]{2,1,0:T(8,128)(2,1)S(1)} %broadcast_in_dim.85), channel_id=1, replica_groups=mesh['dp'=64,'tensor'=4] {'tensor'}, dimensions={0} | all-to-all | bytes 4194304 | tf_op jit(solution)/shard_map/all_to_all | solution.py:19
  864.3 226.2 %all-gather.9.cloned.1.call-done = bf16[2048,2560]{1,0:T(8,128)(2,1)} async-done(((bf16[32,2560]{1,0:T(8,128)(2,1)}), bf16[2048,2560]{1,0:T(8,128)(2,1)}) %all-gather.9.cloned.1.call-update) | async-done | bytes 10485776 | tf_op jit(solution)/shard_map/all_gather | solution.py:34
  1090.5 7.8 fusion.30
  1098.3 341.8 %all-gather.11.cloned.1.call-done = bf16[1280,2048]{0,1:T(8,128)(2,1)} async-done(((bf16[1280,32]{0,1:T(8,128)(2,1)}), bf16[1280,2048]{0,1:T(8,128)(2,1)}) %all-gather.11.cloned.1.call-update) | async-done | bytes 5242896 | tf_op jit(solution)/shard_map/all_gather | solution.py:180
  1440.1 13.1 convolution_convert_fusion.1
  1454.2 98.7 %reduce-scatter.2.cloned.1.call-done = bf16[128,2048]{1,0:T(8,128)(2,1)} async-done(((bf16[512,2048]{1,0:T(8,128)(2,1)}), bf16[128,2048]{1,0:T(8,128)(2,1)}) %reduce-scatter.2.cloned.1.call-update) | async-done | bytes 524304 | tf_op jit(solution)/shard_map/reduce_scatter | solution.py:183
  1557.5 4.0 all-to-all-start.3
  1562.2 6.3 all-to-all-done.3
  1570.4 7.6 all-to-all-start.4
  1579.5 7.6 all-to-all-done.4
  (152 shorter events, 73.4 us)
Async XLA Ops:
  7.2 24.5 %copy-start = (f32[32,8]{0,1:T(8,128)S(1)}, f32[32,8]{0,1:T(8,128)}, u32[]{:S(2)}) copy-start(f32[32,8]{0,1:T(8,128)} %param.29) | copy-start | bytes 3076
  7.2 10.2 copy-start.3
  7.2 330.1 %all-gather.5.cloned.1.call-start = ((), (), s32[]{:S(2)}) async-start(), calls=%async_computation.6 | async-start | bytes 6389760 | tf_op jit(solution)/shard_map/all_gather | solution.py:34
  8.8 678.1 %all-gather.7.cloned.1.call-start = ((), (), s32[]{:S(2)}) async-start(), calls=%async_computation.7 | async-start | bytes 2129920 | tf_op jit(solution)/shard_map/all_gather | solution.py:165
  9.5 1080.9 %all-gather.9.cloned.1.call-start = ((), (), s32[]{:S(2)}) async-start(), calls=%async_computation.8 | async-start | bytes 10649600 | tf_op jit(solution)/shard_map/all_gather | solution.py:34
  17.7 0.7 copy-start.4
  21.1 59.3 %all-to-all-start = ((bf16[4,128,2048]{2,1,0:T(8,128)(2,1)}), bf16[4,128,2048]{2,1,0:T(8,128)(2,1)S(1)}, u32[]{:S(2)}, u32[]{:S(2)}) async-start(bf16[4,128,2048]{2,1,0:T(8,128)(2,1)} %broadcast_in_dim.58), calls=%async_computation | async-start | bytes 4194304 | tf_op jit(solution)/shard_map/all_to_all | solution.py:19
  31.1 1409.0 %all-gather.11.cloned.1.call-start = ((), (), s32[]{:S(2)}) async-start(), calls=%async_computation.9 | async-start | bytes 5324800 | tf_op jit(solution)/shard_map/all_gather | solution.py:180
  358.6 1.6 slice-start
  363.1 1.2 slice-start.1
  371.6 1.6 slice-start
  376.1 1.2 slice-start.1
  384.6 1.6 slice-start
  389.1 1.2 slice-start.1
  397.5 1.6 slice-start
  402.0 1.2 slice-start.1
  410.5 1.6 slice-start
  415.0 1.2 slice-start.1
  423.5 1.6 slice-start
  428.0 1.2 slice-start.1
  436.5 1.6 slice-start
  441.0 1.2 slice-start.1
  449.4 1.6 slice-start
  453.9 1.2 slice-start.1
  691.2 124.7 %all-to-all-start.1 = ((bf16[4,128,2048]{2,1,0:T(8,128)(2,1)}), bf16[4,128,2048]{2,1,0:T(8,128)(2,1)}, u32[]{:S(2)}, u32[]{:S(2)}) async-start(bf16[4,128,2048]{2,1,0:T(8,128)(2,1)} %bitcast.15), calls=%async_computation.1 | async-start | bytes 4194304 | tf_op jit(solution)/shard_map/all_to_all | solution.py:45
  777.9 775.0 %reduce-scatter.2.cloned.1.call-start = ((), (), s32[]{:S(2)}) async-start(), calls=%async_computation.10 | async-start | bytes 2621440 | tf_op jit(solution)/shard_map/reduce_scatter | solution.py:183
  818.3 1.2 copy-start.2
  1557.5 11.0 all-to-all-start.3
  1561.5 28.7 %copy-start.1 = (f32[32,8]{0,1:T(8,128)S(1)}, f32[32,8]{0,1:T(8,128)}, u32[]{:S(2)}) copy-start(f32[32,8]{0,1:T(8,128)} %param.29) | copy-start | bytes 3076
  1570.4 16.7 %all-to-all-start.4 = ((f32[64,1,2]{2,1,0:T(1,128)}), f32[64,1,2]{2,1,0:T(1,128)S(1)}, u32[]{:S(2)}, u32[]{:S(2)}) async-start(f32[64,1,2]{2,1,0:T(1,128)} %broadcast_in_dim.88), calls=%async_computation.5 | async-start | bytes 65536 | tf_op jit(solution)/shard_map/all_to_all | solution.py:19
Sparse Core Ops, SparseCore 0:
  10.4 326.9 all-gather.4
  339.1 347.6 all-gather.6
  688.6 401.8 all-gather.8
  1092.1 347.8 all-gather.10
  1453.3 99.5 reduce-scatter.1
where the time goes:
time: 1600 us
  waiting for transfers between devices  1250 us (78%)
  starting transfers between devices  108 us (7%)
  local copies, waits for them, and re-layouts  95.1 us (6%)
  matrix products  63.7 us (4%)
  blocking collectives  44.2 us (3%)
  between operations  18.8 us (1%)
  other arithmetic  16.4 us (1%)
    all_gather x2, waiting for transfers between devices, in_one_piece(): lax.all_gather(both, axis, axis=dim, tiled=True)  483 us
    all_gather x1, waiting for transfers between devices, local(): lax.all_gather(w_down, 'dp', axis=1, tiled=True)  342 us
    all_gather x1, waiting for transfers between devices, local(): lax.all_gather(w_out, 'dp', axis=1, tiled=True)  227 us
    reduce_scatter x1, waiting for transfers between devices, local(): lax.psum_scatter(feed_partial, 'tensor', scatter_dimension=0, tiled=True)  98.7 us
    all_to_all x1, starting transfers between devices, sent_and_summed(): parts = lax.all_to_all(cut_along(array, dim, peers), axis, 0, 0, tiled=True)  86.6 us
    all_to_all x3, waiting for transfers between devices, from_everyone(): lax.all_to_all(jnp.broadcast_to(array[None], (peers, *array.shape)), axis...  62.2 us
    all_to_all x1, blocking collectives, from_everyone(): lax.all_to_all(jnp.broadcast_to(array[None], (peers, *array.shape)), axis...  44.2 us
    all_to_all x1, waiting for transfers between devices, sent_and_summed(): parts = lax.all_to_all(cut_along(array, dim, peers), axis, 0, 0, tiled=True)  36.6 us
  transfers between devices with their start and end apart: 9, of which 9 were waited for; matrix products, arithmetic and copies ran while one was open for 8% of the time, Pallas kernels for 0%

commit v1 on v0

--- a/solution.py
+++ b/solution.py
@@ -162,7 +162,11 @@
     context = lax.map(head_step, (query_heads, key_heads, value_heads, offset_bias))
     context = context.transpose(1, 0, 2).reshape(LEN, inner_width)
     attn_partial = jnp.dot(
-        context, lax.all_gather(w_out, "dp", axis=1, tiled=True), preferred_element_type=jnp.float32
+        context,
+        jnp.concatenate(
+            lax.all_to_all(jnp.stack([w_out] * lax.axis_size("dp")), "dp", 0, 0), axis=1
+        ),
+        preferred_element_type=jnp.float32,
     ).astype(jnp.bfloat16)
     mid_own = own_rows + sent_and_summed(attn_partial, "tensor", 0)
     mid_normed = gather_directly(rms_norm(mid_own, feed_gain).astype(jnp.bfloat16), "tensor", 0)

time: 1600 us -> 1270 us (0.79)
  waiting for transfers between devices: 1250 us -> 926 us
    all_gather x1 -> x0, waiting for transfers between devices: 227 us -> none  [local(): lax.all_gather(w_out, 'dp', axis=1, tiled=True)]
    all_gather x2, waiting for transfers between devices: 483 us -> 373 us  [in_one_piece(): lax.all_gather(both, axis, axis=dim, tiled=True)]
    all_to_all x1, starting transfers between devices: 86.6 us -> 53.6 us  [sent_and_summed(): parts = lax.all_to_all(cut_along(array, dim, peers), axis, 0, 0, tiled=True)]
    all_to_all x0 -> x1, starting transfers between devices: none -> 22.7 us  [local(): lax.all_to_all(jnp.stack([w_out] * lax.axis_size('dp')), 'dp', 0, 0)]
  transfers between devices with their start and end apart: 9 -> 9, of which waited for: 9 -> 8; matrix products, arithmetic and copies ran while one was open for 8% -> 10% of each run, Pallas kernels for 0% -> 0%
where the time goes in v1:
time: 1270 us
  waiting for transfers between devices  926 us (73%)
  starting transfers between devices  98.2 us (8%)
  local copies, waits for them, and re-layouts  96.7 us (8%)
  matrix products  63.7 us (5%)
  blocking collectives  45.5 us (4%)
  between operations  18.8 us (1%)
  other arithmetic  16.4 us (1%)
    all_gather x2, waiting for transfers between devices, in_one_piece(): lax.all_gather(both, axis, axis=dim, tiled=True)  373 us
    all_gather x1, waiting for transfers between devices, local(): lax.all_gather(w_down, 'dp', axis=1, tiled=True)  343 us
    reduce_scatter x1, waiting for transfers between devices, local(): lax.psum_scatter(feed_partial, 'tensor', scatter_dimension=0, tiled=True)  98.7 us
    all_to_all x3, waiting for transfers between devices, from_everyone(): lax.all_to_all(jnp.broadcast_to(array[None], (peers, *array.shape)), axis...  59.2 us
    all_to_all x1, starting transfers between devices, sent_and_summed(): parts = lax.all_to_all(cut_along(array, dim, peers), axis, 0, 0, tiled=True)  53.6 us
    all_to_all x1, waiting for transfers between devices, sent_and_summed(): parts = lax.all_to_all(cut_along(array, dim, peers), axis, 0, 0, tiled=True)  51.9 us
    all_to_all x1, blocking collectives, from_everyone(): lax.all_to_all(jnp.broadcast_to(array[None], (peers, *array.shape)), axis...  45.5 us
  transfers between devices with their start and end apart: 9, of which 8 were waited for; matrix products, arithmetic and copies ran while one was open for 10% of the time, Pallas kernels for 0%

profile of v1, /device:TPU:1, one launch (start us, length us, event | category | flops | bytes accessed | tf_op | source)
XLA Modules:
  0.0 1265.9 jit_solution(7353563323077735729)
XLA Ops:
  20.4 10.1 all-to-all-start
  31.6 45.4 %all-to-all-done = bf16[4,128,2048]{2,1,0:T(8,128)(2,1)S(1)} async-done(((bf16[4,128,2048]{2,1,0:T(8,128)(2,1)}), bf16[4,128,2048]{2,1,0:T(8,128)(2,1)S(1)}, u32[]{:S(2)}, u32[]{:S(2)}) %all-to-all-start) | async-done | bytes 2097184 | tf_op jit(solution)/shard_map/all_to_all | solution.py:19
  78.6 22.7 %all-to-all-start.1 = ((bf16[64,512,32]{1,2,0:T(8,128)(2,1)}), bf16[64,512,32]{1,2,0:T(8,128)(2,1)}, u32[]{:S(2)}, u32[]{:S(2)}) async-start(bf16[64,512,32]{1,2,0:T(8,128)(2,1)} %stack.2), calls=%async_computation.1 | async-start | bytes 4194304 | tf_op jit(solution)/shard_map/all_to_all | solution.py:167
  101.4 245.4 %all-gather.4.cloned.1.call-done = bf16[2048,1536]{1,0:T(8,128)(2,1)} async-done(((bf16[32,1536]{1,0:T(8,128)(2,1)}), bf16[2048,1536]{1,0:T(8,128)(2,1)}) %all-gather.4.cloned.1.call-update) | async-done | bytes 6291472 | tf_op jit(solution)/shard_map/all_gather | solution.py:34
  346.8 3.7 fusion.39
  350.5 2.4 copy.44
  352.9 3.7 fusion.42
  356.6 2.3 copy.45
  358.9 3.7 fusion.45
  362.6 2.4 copy.46
  365.1 103.9 %while.11 = (s32[]{:T(128)}, bf16[8,512,64]{1,2,0:T(8,128)(2,1)}, bf16[8,512,64]{2,1,0:T(8,128)(2,1)}, bf16[8,512,64]{2,1,0:T(8,128)(2,1)}, f32[8,1023]{1,0:T(8,...) while((s32[]{:T(128)}, bf16[8,512,64]{1,2,0:T(8,128)(2,1)}, ...), condition=%wide.region_4.7_spmd.clone, body=%wide.region_1.6_spmd.clone.sunk | while | flops 69238272 | bytes 26672264 | solution.py:162
  365.3 2.7 tile.17
  369.6 2.9 reshape.337
  376.2 1.8 fusion.90
  378.3 2.7 tile.17
  382.6 2.9 reshape.337
  391.3 2.7 tile.17
  395.5 2.9 reshape.337
  402.1 1.8 fusion.90
  404.3 2.7 tile.17
  408.5 2.9 reshape.337
  415.1 1.8 fusion.90
  417.2 2.7 tile.17
  421.5 2.9 reshape.337
  428.1 1.8 fusion.90
  430.2 2.7 tile.17
  434.5 2.9 reshape.337
  441.1 1.8 fusion.90
  443.2 2.7 tile.17
  447.5 2.9 reshape.337
  454.1 1.8 fusion.90
  456.2 2.7 tile.17
  460.5 2.9 reshape.337
  467.1 1.8 fusion.90
  468.9 4.4 convolution_convert_fusion.2
  473.4 53.6 %all-to-all-start.2 = ((bf16[4,128,2048]{2,1,0:T(8,128)(2,1)}), bf16[4,128,2048]{2,1,0:T(8,128)(2,1)}, u32[]{:S(2)}, u32[]{:S(2)}) async-start(bf16[4,128,2048]{2,1,0:T(8,128)(2,1)} %bitcast.17), calls=%async_computation.2 | async-start | bytes 4194304 | tf_op jit(solution)/shard_map/all_to_all | solution.py:45
  528.4 51.9 %all-to-all-done.2 = bf16[4,128,2048]{2,1,0:T(8,128)(2,1)} async-done(((bf16[4,128,2048]{2,1,0:T(8,128)(2,1)}), bf16[4,128,2048]{2,1,0:T(8,128)(2,1)}, u32[]{:S(2)}, u32[]{:S(2)}) %all-to-all-start.2) | async-done | bytes 2097184 | tf_op jit(solution)/shard_map/all_to_all | solution.py:45
  580.2 2.1 convert_reduce_fusion
  584.4 45.5 %all_to_all.32 = bf16[4,128,2048]{2,1,0:T(8,128)(2,1)} all-to-all(bf16[4,128,2048]{2,1,0:T(8,128)(2,1)S(1)} %broadcast_in_dim.85), channel_id=1, replica_groups=mesh['dp'=64,'tensor'=4] {'tensor'}, dimensions={0} | all-to-all | bytes 4194304 | tf_op jit(solution)/shard_map/all_to_all | solution.py:19
  629.8 127.9 %all-gather.6.cloned.1.call-done = bf16[2048,2560]{1,0:T(8,128)(2,1)} async-done(((bf16[32,2560]{1,0:T(8,128)(2,1)}), bf16[2048,2560]{1,0:T(8,128)(2,1)}) %all-gather.6.cloned.1.call-update) | async-done | bytes 10485776 | tf_op jit(solution)/shard_map/all_gather | solution.py:34
  757.7 7.8 fusion.30
  765.6 342.5 %all-gather.8.cloned.1.call-done = bf16[1280,2048]{0,1:T(8,128)(2,1)} async-done(((bf16[1280,32]{0,1:T(8,128)(2,1)}), bf16[1280,2048]{0,1:T(8,128)(2,1)}) %all-gather.8.cloned.1.call-update) | async-done | bytes 5242896 | tf_op jit(solution)/shard_map/all_gather | solution.py:184
  1108.1 13.1 %convolution_convert_fusion.1 = bf16[512,2048]{1,0:T(8,128)(2,1)} fusion(bf16[1280,2048]{0,1:T(8,128)(2,1)} %all-gather.8.cloned.1.call-done, f32[512,1280]{1,0:T(8,128)} %fusion.30, bf16[512,2048]{1,0:T(8,128)(2,1)} %bitcast.94, bf16[2048,2560]{1,0:T(8,128)(2,1)} %all-gather.6.cloned.1.call-done), kind=kOutput, calls=%fused_computation.33 | convolution fusion | flops 5371068416 | bytes 17301504 | tf_op jit(solution)/shard_map/dot_general | solution.py:182
  1122.2 98.7 %reduce-scatter.2.cloned.1.call-done = bf16[128,2048]{1,0:T(8,128)(2,1)} async-done(((bf16[512,2048]{1,0:T(8,128)(2,1)}), bf16[128,2048]{1,0:T(8,128)(2,1)}) %reduce-scatter.2.cloned.1.call-update) | async-done | bytes 524304 | tf_op jit(solution)/shard_map/reduce_scatter | solution.py:187
  1225.5 4.0 all-to-all-start.4
  1230.2 6.3 all-to-all-done.4
  1238.4 7.6 all-to-all-start.5
  1247.5 7.6 all-to-all-done.5
  (154 shorter events, 74.5 us)
Async XLA Ops:
  7.2 24.0 %copy-start = (f32[32,8]{0,1:T(8,128)S(1)}, f32[32,8]{0,1:T(8,128)}, u32[]{:S(2)}) copy-start(f32[32,8]{0,1:T(8,128)} %param.29) | copy-start | bytes 3076
  7.2 9.4 copy-start.3
  7.2 339.6 %all-gather.4.cloned.1.call-start = ((), (), s32[]{:S(2)}) async-start(), calls=%async_computation.7 | async-start | bytes 6389760 | tf_op jit(solution)/shard_map/all_gather | solution.py:34
  8.8 749.0 %all-gather.6.cloned.1.call-start = ((), (), s32[]{:S(2)}) async-start(), calls=%async_computation.8 | async-start | bytes 10649600 | tf_op jit(solution)/shard_map/all_gather | solution.py:34
  16.9 0.7 copy-start.5
  20.3 56.7 %copy-start.4 = (bf16[512,32]{0,1:T(8,128)(2,1)S(1)}, bf16[512,32]{0,1:T(8,128)(2,1)}, u32[]{:S(2)}) copy-start(bf16[512,32]{0,1:T(8,128)(2,1)} %param.28) | copy-start | bytes 98308
  20.4 56.7 %all-to-all-start = ((bf16[4,128,2048]{2,1,0:T(8,128)(2,1)}), bf16[4,128,2048]{2,1,0:T(8,128)(2,1)S(1)}, u32[]{:S(2)}, u32[]{:S(2)}) async-start(bf16[4,128,2048]{2,1,0:T(8,128)(2,1)} %broadcast_in_dim.58), calls=%async_computation | async-start | bytes 4194304 | tf_op jit(solution)/shard_map/all_to_all | solution.py:19
  30.4 1077.7 %all-gather.8.cloned.1.call-start = ((), (), s32[]{:S(2)}) async-start(), calls=%async_computation.9 | async-start | bytes 5324800 | tf_op jit(solution)/shard_map/all_gather | solution.py:184
  78.6 390.3 %all-to-all-start.1 = ((bf16[64,512,32]{1,2,0:T(8,128)(2,1)}), bf16[64,512,32]{1,2,0:T(8,128)(2,1)}, u32[]{:S(2)}, u32[]{:S(2)}) async-start(bf16[64,512,32]{1,2,0:T(8,128)(2,1)} %stack.2), calls=%async_computation.1 | async-start | bytes 4194304 | tf_op jit(solution)/shard_map/all_to_all | solution.py:167
  368.0 1.6 slice-start
  372.5 1.2 slice-start.1
  381.0 1.6 slice-start
  385.5 1.2 slice-start.1
  393.9 1.6 slice-start
  398.4 1.2 slice-start.1
  406.9 1.6 slice-start
  411.4 1.2 slice-start.1
  419.9 1.6 slice-start
  424.4 1.2 slice-start.1
  432.9 1.6 slice-start
  437.4 1.2 slice-start.1
  445.9 1.6 slice-start
  450.4 1.2 slice-start.1
  458.9 1.6 slice-start
  463.4 1.2 slice-start.1
  473.4 106.9 %all-to-all-start.2 = ((bf16[4,128,2048]{2,1,0:T(8,128)(2,1)}), bf16[4,128,2048]{2,1,0:T(8,128)(2,1)}, u32[]{:S(2)}, u32[]{:S(2)}) async-start(bf16[4,128,2048]{2,1,0:T(8,128)(2,1)} %bitcast.17), calls=%async_computation.2 | async-start | bytes 4194304 | tf_op jit(solution)/shard_map/all_to_all | solution.py:45
  527.0 693.9 %reduce-scatter.2.cloned.1.call-start = ((), (), s32[]{:S(2)}) async-start(), calls=%async_computation.10 | async-start | bytes 2621440 | tf_op jit(solution)/shard_map/reduce_scatter | solution.py:187
  582.7 1.2 copy-start.2
  1225.5 11.0 all-to-all-start.4
  1229.5 28.7 %copy-start.1 = (f32[32,8]{0,1:T(8,128)S(1)}, f32[32,8]{0,1:T(8,128)}, u32[]{:S(2)}) copy-start(f32[32,8]{0,1:T(8,128)} %param.29) | copy-start | bytes 3076
  1238.4 16.7 %all-to-all-start.5 = ((f32[64,1,2]{2,1,0:T(1,128)}), f32[64,1,2]{2,1,0:T(1,128)S(1)}, u32[]{:S(2)}, u32[]{:S(2)}) async-start(f32[64,1,2]{2,1,0:T(1,128)} %broadcast_in_dim.88), calls=%async_computation.6 | async-start | bytes 65536 | tf_op jit(solution)/shard_map/all_to_all | solution.py:19
Sparse Core Ops, SparseCore 0:
  10.4 336.4 all-gather.3
  348.6 409.0 all-gather.5
  759.5 348.4 all-gather.7
  1121.4 99.5 reduce-scatter.1
